TPU v7x, 32 devices: a whole 2x2x4 slice. The times are simulated.
32 devices in a mesh: blk: 8 (over z, y), batch: 4 (over x, core).
Axes of the slice: x: 2, y: 2, z: 4, core: 2. Of those that a mesh axis runs over, the one named last changes fastest.
Arguments:
- coefficients: bfloat16 [120, 24576], P(None, ('blk', 'batch')), may hold values from -6 to 6
- transforms: bfloat16 [12, 24, 24576], P(None, 'batch', 'blk'), may hold values from -6 to 6
- basis: bfloat16 [120, 3, 4096], P(None, None, 'blk'), may hold values from -0.5 to 0.5
- template: bfloat16 [3, 4096], P(None, 'blk'), may hold values from -6 to 6
- skin_weights: bfloat16 [24, 4096], P(None, 'blk'), may hold values from 0.019897461 to 1
Outputs:
- skinned: bfloat16 [24576, 4, 3, 512], P(('blk', 'batch'))
All inputs are finite; a program needn't handle non-finite values.
Results may differ from a plain program's by a relative error of at most 0.0049.
Values may be sent and summed in bfloat16 or wider, within the bound.
A program may use at most 192 MiB of HBM per device.

v0:
```python
import functools
import jax
import jax.numpy as jnp
from jax import lax
from jax.experimental import pallas as pl
from jax.experimental.pallas import tpu as pltpu
from jax.sharding import PartitionSpec as P

STEPS = 4
LANES = 128
BF16 = jnp.bfloat16
F32 = jnp.float32


def exchange_kernel(
    n_blk, n_batch, tr_ref, ba_ref, te_ref, we_ref,
    tr_out, ba_out, te_out, we_out,
    stage, tr_send, tr_recv, bl_send, bl_recv, fw_send, fw_recv, own_sem,
):
    blk, bat = lax.axis_index("blk"), lax.axis_index("batch")
    sibling = bat + 1 - 2 * lax.rem(bat, 2)
    odd = lax.rem(blk, 2)
    pair = blk + 1 - 2 * odd
    after = lax.rem(blk + 2, n_blk)
    before = lax.rem(blk + n_blk - 2, n_blk)
    chars = tr_out.shape[3]
    half = ba_ref.shape[2] // 2

    own = pltpu.make_async_copy(
        tr_ref.at[:, :, pl.ds(pl.multiple_of(bat * chars, LANES), chars)], stage, own_sem.at[0]
    )
    own.start()

    partners = [lax.rem(bat + i, n_batch) for i in range(1, n_batch)]
    barrier = pltpu.get_barrier_semaphore()
    for q in partners:
        pl.semaphore_signal(barrier, inc=1, device_id={"blk": blk, "batch": q})
    for b in (pair, after, before):
        pl.semaphore_signal(barrier, inc=1, device_id={"blk": b, "batch": bat})
    pl.semaphore_wait(barrier, len(partners) + 3)

    mine = pl.ds(pl.multiple_of(lax.rem(bat, 2) * half, LANES), half)
    pieces = [((te_ref, te_out), (we_ref, we_out), (ba_ref.at[0], ba_out.at[:, 0]))]
    pieces += [((ba_ref.at[e], ba_out.at[:, e]),) for e in range(1, ba_ref.shape[0])]

    def hop(slot_from, slot_to, piece, where, send, recv, target):
        made = []
        for k, (src, dst) in enumerate(pieces[piece]):
            at = piece + k if piece == 0 else piece + 2
            lead = (slice(None),) * (len(src.shape) - 1)
            part = src.at[lead + (mine,)] if slot_from == 0 else dst.at[(slot_from - 1,) + lead + (mine,)]
            made.append(pltpu.make_async_remote_copy(
                src_ref=part, dst_ref=dst.at[(slot_to - 1,) + lead + (mine,)],
                send_sem=send.at[where, at], recv_sem=recv.at[slot_to - 1, at],
                device_id={"blk": target[0], "batch": target[1]},
            ))
        return made

    def start(copies):
        for c in copies:
            c.start()

    def first_hop(piece):
        return hop(0, 2, piece, 1, bl_send, bl_recv, (after, bat))

    def to_odd(piece):
        return hop(0, 1, piece, 0, bl_send, bl_recv, (pair, bat))

    def odd_forward(piece):
        return hop(2, 1, piece, 0, bl_send, bl_recv, (pair, bat))

    def even_forward(piece):
        return hop(2, 3, piece, 2, bl_send, bl_recv, (pair, bat))

    def even_onward(piece):
        return hop(1, 3, piece, 3, bl_send, bl_recv, (after, bat))

    def share(slot, piece):
        return hop(slot, slot, piece, slot - 1, fw_send, fw_recv, (blk, sibling))

    def take(slot, piece):
        for c in hop(slot, slot, piece, slot - 1, bl_send, bl_recv, (pair, bat)):
            c.wait_recv()
        if slot == 2:
            @pl.when(odd == 0)
            def _():
                start(even_forward(piece))

            @pl.when(odd == 1)
            def _():
                start(odd_forward(piece))
        if slot == 1:
            @pl.when(odd == 0)
            def _():
                start(even_onward(piece))
        start(share(slot, piece))

    count = len(pieces)
    for p in range(count):
        start(first_hop(p))

    moves = []
    for i, q in enumerate(partners):
        moves.append(pltpu.make_async_remote_copy(
            src_ref=tr_ref.at[:, :, pl.ds(pl.multiple_of(q * chars, LANES), chars)],
            dst_ref=tr_out.at[bat],
            send_sem=tr_send.at[i], recv_sem=tr_recv.at[i],
            device_id={"blk": blk, "batch": q},
        ))
    start(moves)

    @pl.when(odd == 0)
    def _():
        for p in range(count):
            start(to_odd(p))

    own.wait()
    put = pltpu.make_async_copy(stage, tr_out.at[bat], own_sem.at[1])
    put.start()

    for step in range(count + 2):
        for slot, late in ((2, 0), (1, 1), (3, 2)):
            if 0 <= step - late < count:
                take(slot, step - late)

    put.wait()
    for c in moves:
        c.wait()
    for p in range(count):
        for slot in (2, 1, 3):
            for c in share(slot, p):
                c.wait()
        for c in first_hop(p) + to_odd(p):
            c.wait_send()

        @pl.when(odd == 0)
        def _():
            for c in even_forward(p) + even_onward(p):
                c.wait_send()


def exchange(n_blk, n_batch, transforms, basis, template, weights):
    m, jl, total = transforms.shape
    chars = total // n_batch
    hop = STEPS - 1
    assert n_blk % 2 == 0 and n_blk > STEPS and n_batch % 2 == 0 and STEPS == 4
    any_spec = pl.BlockSpec(memory_space=pl.ANY)
    hbm_spec = pl.BlockSpec(memory_space=pl.ANY)
    dma = pltpu.SemaphoreType.DMA
    return pl.pallas_call(
        functools.partial(exchange_kernel, n_blk, n_batch),
        out_shape=(
            jax.ShapeDtypeStruct((n_batch, m, jl, chars), BF16),
            jax.ShapeDtypeStruct((hop,) + basis.shape, BF16),
            jax.ShapeDtypeStruct((hop,) + template.shape, BF16),
            jax.ShapeDtypeStruct((hop,) + weights.shape, BF16),
        ),
        in_specs=[hbm_spec] * 4,
        out_specs=(any_spec,) * 4,
        scratch_shapes=[
            pltpu.VMEM((m, jl, chars), BF16),
            dma((n_batch - 1,)), dma((n_batch - 1,)),
            dma((hop + 1, 5)), dma((hop, 5)), dma((hop, 5)), dma((hop, 5)), dma((2,)),
        ],
        compiler_params=pltpu.CompilerParams(
            collective_id=0, has_side_effects=True, vmem_limit_bytes=67043328
        ),
        cost_estimate=pl.CostEstimate(flops=0, bytes_accessed=20 << 20, transcendentals=0),
        name="exchange",
    )(transforms, basis, template, weights)


def skin_kernel(
    co_ref, tr_ref, ba0_ref, te0_ref, we0_ref, ba_ref, te_ref, we_ref, out_ref,
    basis, weights, mixed0, mixed1, mixed2, shaped, poses, coefs,
):
    rows = co_ref.shape[1]
    k = co_ref.shape[0]
    depth = basis.shape[2]
    comps = poses.shape[0]
    joints = weights.shape[1]
    verts = we0_ref.shape[1]
    tiles = verts // LANES
    wide = 2 * LANES

    @pl.when(pl.program_id(0) == 0)
    def _():
        for s in range(STEPS):
            w = (we0_ref[...] if s == 0 else we_ref[s - 1]).astype(F32)
            weights[s] = (w / jnp.sum(w, axis=0, keepdims=True)).astype(BF16)
            te = te0_ref[...] if s == 0 else te_ref[s - 1]
            for e in range(3):
                basis[s, e, :k] = ba0_ref[e] if s == 0 else ba_ref[s - 1, e]
                row = te[e:e + 1].astype(F32)
                pad = jnp.broadcast_to(row, (depth - k, verts))
                first = lax.broadcasted_iota(jnp.int32, (depth - k, verts), 0) == 0
                basis[s, e, k:] = jnp.where(first, pad, 0.0).astype(BF16)

    ones = jnp.where(
        lax.broadcasted_iota(jnp.int32, (depth - k, rows), 0) == 0, 1.0, 0.0
    ).astype(F32)
    padded = jnp.concatenate([co_ref[...].astype(F32), ones], axis=0)
    coefs[...] = padded.T.astype(BF16)
    for m in range(comps):
        parts = [tr_ref[i, m].astype(F32) for i in range(tr_ref.shape[0])]
        poses[m] = jnp.concatenate(parts, axis=0).T.astype(BF16)

    group = tiles * STEPS
    halves = verts // wide
    for s in range(STEPS):
        for n in range(halves):
            for e in range(3):
                shaped[s, n, e] = jnp.dot(
                    coefs[...], basis[s, e, :, n * wide:(n + 1) * wide],
                    preferred_element_type=F32,
                )
    for d, mixed in enumerate((mixed0, mixed1, mixed2)):
        for s in range(STEPS):
            for n in range(halves):
                w = weights[s, :, n * wide:(n + 1) * wide]
                total = jnp.dot(poses[4 * d + 3], w, preferred_element_type=F32)
                for e in range(3):
                    total = total + shaped[s, n, e] * jnp.dot(
                        poses[4 * d + e], w, preferred_element_type=F32
                    )
                for h in range(wide // LANES):
                    at = (n * (wide // LANES) + h) * STEPS + s
                    mixed[pl.ds(at, rows, stride=group), :] = total[:, h * LANES:(h + 1) * LANES]
        out_ref[:, d] = mixed[...].reshape(rows, group, LANES).astype(BF16)


def skin(coefficients, poses, basis, template, weights, basis_in, template_in, weights_in):
    k, chars = coefficients.shape
    n_batch, comps, jl, _ = poses.shape
    verts = weights.shape[1]
    joints = weights.shape[0]
    rows = LANES
    depth = -(-(k + 1) // 8) * 8
    group = (verts // LANES) * STEPS

    def whole(a):
        return pl.BlockSpec(a.shape, lambda i: (0,) * a.ndim)

    out = pl.pallas_call(
        skin_kernel,
        grid=(chars // rows,),
        out_shape=jax.ShapeDtypeStruct((chars, 3, group, LANES), BF16),
        in_specs=[
            pl.BlockSpec((k, rows), lambda i: (0, i)),
            pl.BlockSpec((n_batch, comps, jl, rows), lambda i: (0, 0, 0, i)),
            whole(basis), whole(template), whole(weights),
            whole(basis_in), whole(template_in), whole(weights_in),
        ],
        out_specs=pl.BlockSpec((rows, 3, group, LANES), lambda i: (i, 0, 0, 0)),
        scratch_shapes=[
            pltpu.VMEM((STEPS, 3, depth, verts), BF16),
            pltpu.VMEM((STEPS, joints, verts), BF16),
            pltpu.VMEM((rows * group, LANES), F32),
            pltpu.VMEM((rows * group, LANES), F32),
            pltpu.VMEM((rows * group, LANES), F32),
            pltpu.VMEM((STEPS, verts // (2 * LANES), 3, rows, 2 * LANES), F32),
            pltpu.VMEM((comps, rows, joints), BF16),
            pltpu.VMEM((rows, depth), BF16),
        ],
        compiler_params=pltpu.CompilerParams(
            dimension_semantics=("arbitrary",), vmem_limit_bytes=67043328
        ),
        name="skin",
    )(coefficients, poses, basis, template, weights, basis_in, template_in, weights_in)
    out = out.reshape(chars, 3, verts // LANES, STEPS, LANES)
    return out.transpose(0, 3, 1, 2, 4).reshape(chars, STEPS, 3, verts)


def solution(mesh):
    n_blk, n_batch = mesh.shape["blk"], mesh.shape["batch"]

    def per_device(coefficients, transforms, basis, template, skin_weights):
        basis = jnp.transpose(basis, (1, 0, 2))
        poses, basis_in, template_in, weights_in = exchange(
            n_blk, n_batch, transforms, basis, template, skin_weights
        )
        return skin(
            coefficients, poses, basis, template, skin_weights,
            basis_in, template_in, weights_in,
        )

    in_specs = (
        P(None, ("blk", "batch")),
        P(None, "batch", "blk"),
        P(None, None, "blk"),
        P(None, "blk"),
        P(None, "blk"),
    )
    out_specs = P(("blk", "batch"), None, None, None)
    return jax.shard_map(
        per_device, mesh=mesh, in_specs=in_specs, out_specs=out_specs, check_vma=False
    )
```

profile of v0, /device:TPU:0, one launch (start us, length us, event | category | flops | bytes accessed | tf_op | source)
XLA Modules:
  0.0 42.1 jit_solution(9025466826308527941)
XLA Ops:
  0.0 22.5 %exchange.1 = (bf16[4,12,6,768]{3,2,1,0:T(8,128)(2,1)}, bf16[3,3,120,512]{3,2,1,0:T(8,128)(2,1)}, bf16[3,3,512]{2,1,0:T(4,128)(2,1)}, bf16[3,24,512]{2,1,0:T(8,128)(2,1)}) custom-call(bf16[12,6,3072]{2,1,0:T(8,128)(2,1)} %tr_ref.1, bf16[3,120,512]{2,1,0:T(8,128)(2,1)} %bitcast.6, bf16[3,512]{1,0:T(4,128)(2,1)} %te0_ref.1, bf16[24,512]{1,0:T(8,128)(2,1)} %we0_ref.1), custom_call_target="tpu_custom_call" | custom-call | bytes 20971520 | tf_op jit(solution)/shard_map/exchange/pallas_call | solution.py:150
  22.5 19.6 %skin.1 = bf16[768,3,16,128]{3,2,1,0:T(8,128)(2,1)} custom-call(bf16[120,768]{1,0:T(8,128)(2,1)} %co_ref.1, bf16[4,12,6,768]{3,2,1,0:T(8,128)(2,1)} %get-tuple-element.9.tr_ref, bf16[3,120,512]{2,1,0:T(8,128)(2,1)} %bitcast.7, bf16[3,512]{1,0:T(4,128)(2,1)} %te0_ref.1, bf16[24,512]{1,0:T(8,128)(2,1)} %we0_ref.1, ...), custom_call_target="tpu_custom_call" | custom-call | tf_op jit(solution)/shard_map/skin/pallas_call | solution.py:244
where the time goes:
time: 42.3 us; the launch traced here: 42.1 us
  Pallas kernels  42.1 us (100%)
    pallas_call x1, Pallas kernels, exchange(): pl.pallas_call(functools.partial(exchange_kernel, n_blk, n_batch), out_sh...  22.5 us
    pallas_call x1, Pallas kernels, skin(): pl.pallas_call(skin_kernel, grid=(chars // rows,), out_shape=jax.ShapeDty...  19.6 us

commit v1 on v0

v1 whole, which is shorter than its diff:
```python
import functools
import jax
import jax.numpy as jnp
from jax import lax
from jax.experimental import pallas as pl
from jax.experimental.pallas import tpu as pltpu
from jax.sharding import PartitionSpec as P

STEPS = 4
LANES = 128
WIDE = 256
ROWS = 128
SLOT = 8
PITCH = 20
BF16 = jnp.bfloat16
F32 = jnp.float32
LAST = STEPS - 1


def place_weights(raw, n_batch, wv):
    joints, verts = raw.shape
    jl = joints // n_batch
    w = raw[...].astype(F32)
    w = (w / jnp.sum(w, axis=0, keepdims=True)).astype(BF16).astype(F32)
    gap = jnp.zeros((SLOT - jl, verts), F32)
    parts = []
    for i in range(n_batch):
        parts += [w[i * jl:(i + 1) * jl], gap]
    packed = jnp.concatenate(parts, axis=0).astype(BF16)
    span = n_batch * SLOT
    for q in range(4):
        wv[q, q * span:(q + 1) * span, :] = packed


def skin_rows(step, coefs, poses, basis, te, wv, mixed):
    k, verts = basis.shape[1], basis.shape[2]
    co = coefs[:, :k]
    ps = [poses[d] for d in range(3)]
    for n in range(verts // WIDE):
        cols = slice(n * WIDE, (n + 1) * WIDE)
        shaped = [
            jnp.dot(co, basis[e, :, cols], preferred_element_type=F32) + te[e:e + 1, cols].astype(F32)
            for e in range(3)
        ]
        for d in range(3):
            total = jnp.dot(ps[d], wv[3, :, cols], preferred_element_type=F32)
            for e in range(3):
                total = total + shaped[e] * jnp.dot(ps[d], wv[e, :, cols], preferred_element_type=F32)
            for h in range(WIDE // LANES):
                g = (n * (WIDE // LANES) + h) * STEPS + step
                at = 2 * (g % 8) + g // 8
                mixed(d, at, total[:, h * LANES:(h + 1) * LANES])


def front_kernel(
    n_blk, n_batch, co_ref, tr_ref, ba_ref, te_ref, we_ref,
    mix, co_t, po_t, bas, tes, wes,
    cov, stage, trv, wv, tr_send, tr_recv, bl_send, bl_recv, fw_send, fw_recv, own_sem,
):
    blk, bat = lax.axis_index("blk"), lax.axis_index("batch")
    sibling = bat + 1 - 2 * lax.rem(bat, 2)
    odd = lax.rem(blk, 2)
    pair = blk + 1 - 2 * odd
    after = lax.rem(blk + 2, n_blk)
    before = lax.rem(blk + n_blk - 2, n_blk)
    chars = trv.shape[3]
    chunks = chars // ROWS
    comps = trv.shape[1]
    jl = trv.shape[2]
    k = cov.shape[0]
    half = bas.shape[3] // 2

    def rows_of(q, c):
        return pl.ds(pl.multiple_of(q * chars + c * ROWS, LANES), ROWS)

    own = [
        pltpu.make_async_copy(tr_ref, stage, own_sem.at[0]),
        pltpu.make_async_copy(ba_ref, bas.at[0], own_sem.at[1]),
        pltpu.make_async_copy(we_ref, wes.at[0], own_sem.at[2]),
        pltpu.make_async_copy(te_ref, tes.at[0], own_sem.at[3]),
        pltpu.make_async_copy(co_ref, cov, own_sem.at[4]),
        pltpu.make_async_copy(
            tr_ref.at[:, :, pl.ds(pl.multiple_of(bat * chars, LANES), chars)], trv.at[bat], own_sem.at[5]
        ),
    ]
    for c in own:
        c.start()

    partners = [lax.rem(bat + i, n_batch) for i in range(1, n_batch)]
    barrier = pltpu.get_barrier_semaphore()
    for q in partners:
        pl.semaphore_signal(barrier, inc=1, device_id={"blk": blk, "batch": q})
    for b in (pair, after, before):
        pl.semaphore_signal(barrier, inc=1, device_id={"blk": b, "batch": bat})

    wv[...] = jnp.zeros_like(wv)

    mine = pl.ds(pl.multiple_of(lax.rem(bat, 2) * half, LANES), half)
    pieces = [
        [tes, wes, (bas, 0)],
        [(bas, 1)],
        [(bas, 2)],
    ]
    count = len(pieces)

    def part(entry, slot):
        if isinstance(entry, tuple):
            return entry[0].at[slot, entry[1], :, mine]
        return entry.at[slot, :, mine]

    def hop(slot_from, slot_to, piece, where, send, recv, target):
        made = []
        for i, entry in enumerate(pieces[piece]):
            at = i if piece == 0 else piece + 2
            made.append(pltpu.make_async_remote_copy(
                src_ref=part(entry, slot_from), dst_ref=part(entry, slot_to),
                send_sem=send.at[where, at], recv_sem=recv.at[slot_to - 1, at],
                device_id={"blk": target[0], "batch": target[1]},
            ))
        return made

    def start(copies):
        for c in copies:
            c.start()

    def first_hop(piece):
        return hop(0, 2, piece, 1, bl_send, bl_recv, (after, bat))

    def to_odd(piece):
        return hop(0, 1, piece, 0, bl_send, bl_recv, (pair, bat))

    def odd_forward(piece):
        return hop(2, 1, piece, 0, bl_send, bl_recv, (pair, bat))

    def even_forward(piece):
        return hop(2, 3, piece, 2, bl_send, bl_recv, (pair, bat))

    def even_onward(piece):
        return hop(1, 3, piece, 3, bl_send, bl_recv, (after, bat))

    def share(slot, piece):
        return hop(slot, slot, piece, slot - 1, fw_send, fw_recv, (blk, sibling))

    def take(slot, piece):
        for c in hop(slot, slot, piece, slot - 1, bl_send, bl_recv, (pair, bat)):
            c.wait_recv()
        if slot == 2:
            @pl.when(odd == 0)
            def _():
                start(even_forward(piece))

            @pl.when(odd == 1)
            def _():
                start(odd_forward(piece))
        if slot == 1:
            @pl.when(odd == 0)
            def _():
                start(even_onward(piece))
        start(share(slot, piece))

    def shared(slot):
        for p in range(count):
            for c in share(slot, p):
                c.wait_recv()

    moves = [[] for _ in range(chunks)]
    for c in range(chunks):
        for i, q in enumerate(partners):
            moves[c].append(pltpu.make_async_remote_copy(
                src_ref=stage.at[:, :, rows_of(q, c)],
                dst_ref=trv.at[bat, :, :, pl.ds(c * ROWS, ROWS)],
                send_sem=tr_send.at[c, i], recv_sem=tr_recv.at[c, i],
                device_id={"blk": blk, "batch": q},
            ))

    pl.semaphore_wait(barrier, len(partners) + 3)
    own[0].wait()
    start(moves[0])
    for c in own[1:4]:
        c.wait()
    for p in range(count):
        start(first_hop(p))

    @pl.when(odd == 0)
    def _():
        for p in range(count):
            start(to_odd(p))

    for c in range(1, chunks):
        start(moves[c])

    place_weights(wes.at[0], n_batch, wv.at[0])
    own[4].wait()
    rest = jnp.zeros((LANES - k, ROWS), F32)
    for c in range(chunks):
        block = jnp.concatenate([cov[:, c * ROWS:(c + 1) * ROWS].astype(F32), rest], axis=0)
        co_t[c] = block.T.astype(BF16)
    own[5].wait()

    gap = jnp.zeros((SLOT - jl, ROWS), F32)

    def turn(c):
        for d in range(3):
            parts = []
            for q in range(4):
                for i in range(n_batch):
                    parts += [trv[i, 4 * d + q, :, c * ROWS:(c + 1) * ROWS].astype(F32), gap]
            po_t[d, c] = jnp.concatenate(parts, axis=0).T.astype(BF16)

    def unit(step, c):
        def put(d, at, value):
            mix[d, c, pl.ds(at, ROWS, stride=PITCH), :] = value
        skin_rows(
            step, co_t.at[c], [po_t[d, c] for d in range(3)], bas.at[step], tes.at[step], wv.at[step], put
        )

    def early(c):
        for i in range(n_batch - 1):
            moves[c][i].wait_recv()
        turn(c)
        unit(0, c)

    early(0)
    early(1)
    take(2, 0)
    early(2)
    take(2, 1)
    early(3)
    take(2, 2)
    early(4)
    take(1, 0)
    early(5)

    shared(2)
    place_weights(wes.at[2], n_batch, wv.at[2])
    group = 2

    def sweep(step, polls):
        for b in range(chunks // group):
            for c in range(group):
                unit(step, b * group + c)
            if b < len(polls):
                take(*polls[b])

    sweep(2, [(1, 1), (1, 2)])
    shared(1)
    place_weights(wes.at[1], n_batch, wv.at[1])
    sweep(1, [(3, 0), (3, 1)])
    take(3, 2)
    shared(3)

    for c in range(chunks):
        for m in moves[c]:
            m.wait_send()
    for p in range(count):
        for slot in (2, 1, 3):
            for c in share(slot, p):
                c.wait_send()
        for c in first_hop(p) + to_odd(p):
            c.wait_send()

        @pl.when(odd == 0)
        def _():
            for c in even_forward(p) + even_onward(p):
                c.wait_send()


def front(n_blk, n_batch, coefficients, transforms, basis, template, weights):
    comps, jl, total = transforms.shape
    chars = total // n_batch
    chunks = chars // ROWS
    k = coefficients.shape[0]
    verts = weights.shape[1]
    joints = weights.shape[0]
    hop = STEPS - 1
    assert n_blk % 2 == 0 and n_blk > STEPS and n_batch % 2 == 0 and STEPS == 4
    assert chars % ROWS == 0 and k <= LANES and comps == 12
    assert joints == n_batch * jl and jl <= SLOT and 4 * n_batch * SLOT == LANES
    dma = pltpu.SemaphoreType.DMA
    any_spec = pl.BlockSpec(memory_space=pl.ANY)
    vmem_spec = pl.BlockSpec(memory_space=pltpu.VMEM)
    inputs = [
        pltpu.with_memory_space_constraint(a, pltpu.HBM)
        for a in (coefficients, transforms, basis, template, weights)
    ]
    return pl.pallas_call(
        functools.partial(front_kernel, n_blk, n_batch),
        out_shape=(
            pltpu.VMEM((3, chunks, ROWS * PITCH, LANES), F32),
            pltpu.VMEM((chunks, ROWS, LANES), BF16),
            pltpu.VMEM((3, chunks, ROWS, LANES), BF16),
            pltpu.VMEM((STEPS,) + basis.shape, BF16),
            pltpu.VMEM((STEPS,) + template.shape, BF16),
            pltpu.VMEM((STEPS,) + weights.shape, BF16),
        ),
        in_specs=[any_spec] * 5,
        out_specs=(vmem_spec,) * 6,
        scratch_shapes=[
            pltpu.VMEM((k, chars), BF16),
            pltpu.VMEM(transforms.shape, BF16),
            pltpu.VMEM((n_batch, comps, jl, chars), BF16),
            pltpu.VMEM((hop, 4, LANES, verts), BF16),
            dma((chunks, n_batch - 1)), dma((chunks, n_batch - 1)),
            dma((hop + 1, 5)), dma((hop, 5)), dma((hop, 5)), dma((hop, 5)), dma((6,)),
        ],
        compiler_params=pltpu.CompilerParams(
            collective_id=0, has_side_effects=True, vmem_limit_bytes=16 << 20
        ),
        cost_estimate=pl.CostEstimate(flops=0, bytes_accessed=20 << 20, transcendentals=0),
        name="front",
    )(*inputs)


def back_kernel(
    n_batch, mix_in, co_t, po_t, bas, tes, wes, out_ref, mix, wv, staged, sem,
):
    chunks = co_t.shape[0]
    wv[...] = jnp.zeros_like(wv)
    place_weights(wes.at[LAST], n_batch, wv)

    def send(c):
        return pltpu.make_async_copy(
            staged.at[lax.rem(c, 2)], out_ref.at[pl.ds(c * ROWS, ROWS)], sem.at[lax.rem(c, 2)]
        )

    for c in range(chunks):
        def put(d, at, value):
            mix[d, c, pl.ds(at, ROWS, stride=PITCH), :] = value
        skin_rows(
            LAST, co_t.at[c], [po_t[d, c] for d in range(3)], bas.at[LAST], tes.at[LAST], wv, put
        )
        if c >= 2:
            send(c - 2).wait()
        for r in range(ROWS):
            for d in range(3):
                low = mix[d, c, pl.ds(r * PITCH, 8, stride=2), :]
                high = mix[d, c, pl.ds(r * PITCH + 1, 8, stride=2), :]
                staged[c % 2, r, d] = jnp.concatenate([low, high], axis=0).astype(BF16)
        send(c).start()
    for c in range(max(chunks - 2, 0), chunks):
        send(c).wait()


def back(n_batch, mix, co_t, po_t, bas, tes, wes):
    chunks = co_t.shape[0]
    chars = chunks * ROWS
    verts = wes.shape[2]
    group = (verts // LANES) * STEPS
    any_spec = pl.BlockSpec(memory_space=pl.ANY)
    vmem_spec = pl.BlockSpec(memory_space=pltpu.VMEM)
    out, _ = pl.pallas_call(
        functools.partial(back_kernel, n_batch),
        out_shape=(
            jax.ShapeDtypeStruct((chars, 3, group, LANES), BF16),
            pltpu.VMEM(mix.shape, F32),
        ),
        in_specs=[vmem_spec] * 6,
        out_specs=(any_spec, vmem_spec),
        input_output_aliases={0: 1},
        scratch_shapes=[
            pltpu.VMEM((4, LANES, verts), BF16),
            pltpu.VMEM((2, ROWS, 3, group, LANES), BF16),
            pltpu.SemaphoreType.DMA((2,)),
        ],
        compiler_params=pltpu.CompilerParams(vmem_limit_bytes=16 << 20),
        name="back",
    )(mix, co_t, po_t, bas, tes, wes)
    out = out.reshape(chars, 3, verts // LANES, STEPS, LANES)
    return out.transpose(0, 3, 1, 2, 4).reshape(chars, STEPS, 3, verts)


def solution(mesh):
    n_blk, n_batch = mesh.shape["blk"], mesh.shape["batch"]

    def per_device(coefficients, transforms, basis, template, skin_weights):
        basis = jnp.transpose(basis, (1, 0, 2))
        return back(n_batch, *front(
            n_blk, n_batch, coefficients, transforms, basis, template, skin_weights
        ))

    in_specs = (
        P(None, ("blk", "batch")),
        P(None, "batch", "blk"),
        P(None, None, "blk"),
        P(None, "blk"),
        P(None, "blk"),
    )
    out_specs = P(("blk", "batch"), None, None, None)
    return jax.shard_map(
        per_device, mesh=mesh, in_specs=in_specs, out_specs=out_specs, check_vma=False
    )
```

time: 42.3 us -> 31.8 us (0.75)
  Pallas kernels: 42.1 us -> 31.5 us
    pallas_call x2, Pallas kernels: 42.1 us -> 31.5 us  [the longest x1 24.8 us: front(): pl.pallas_call(functools.partial(front_kernel, n_blk, n_batch), out_shape...]
where the time goes in v1:
time: 31.8 us; the launch traced here: 31.7 us
  Pallas kernels  31.5 us (99%)
    pallas_call x1, Pallas kernels, front(): pl.pallas_call(functools.partial(front_kernel, n_blk, n_batch), out_shape...  24.8 us
    pallas_call x1, Pallas kernels, back(): pl.pallas_call(functools.partial(back_kernel, n_batch), out_shape=(jax.Sh...  6.66 us

profile of v1, /device:TPU:0, one launch (start us, length us, event | category | flops | bytes accessed | tf_op | source)
XLA Modules:
  0.0 31.7 jit_solution(2543029792672089132)
XLA Ops:
  0.0 24.8 %front.1 = (f32[3,6,2560,128]{3,2,1,0:T(8,128)S(1)}, bf16[6,128,128]{2,1,0:T(8,128)(2,1)S(1)}, bf16[3,6,128,128]{3,2,1,0:T(8,128)(2,1)S(1)}, bf16[4,3,120,512]{3...) custom-call(bf16[120,768]{1,0:T(8,128)(2,1)} %co_ref.1, ...), custom_call_target="tpu_custom_call" | custom-call | bytes 20971520 | tf_op jit(solution)/shard_map/front/pallas_call | solution.py:286
  24.8 6.7 %back.1 = (bf16[768,3,16,128]{3,2,1,0:T(8,128)(2,1)}, f32[3,6,2560,128]{3,2,1,0:T(8,128)S(1)}) custom-call(f32[3,6,2560,128]{3,2,1,0:T(8,128)S(1)} %get-tuple-element.12.mix_in, bf16[6,128,128]{2,1,0:T(8,128)(2,1)S(1)} %get-tuple-element.13.co_t, bf16[3,6,128,128]{3,2,1,0:T(8,128)(2,1)S(1)} %get-tuple-element.14.po_t, ...), custom_call_target="tpu_custom_call", output_to_operand_aliasing={{1}: (0, {})} | custom-call | tf_op jit(solution)/shard_map/back/pallas_call | solution.py:351

commit v2 on v1

v2 whole, which is shorter than its diff:
```python
import functools
import jax
import jax.numpy as jnp
from jax import lax
from jax.experimental import pallas as pl
from jax.experimental.pallas import tpu as pltpu
from jax.sharding import PartitionSpec as P

STEPS = 4
LANES = 128
WIDE = 256
ROWS = 128
PITCH = 20
PARTS = 2
CUT = 64
BF16 = jnp.bfloat16
F32 = jnp.float32
LAST = STEPS - 1


def place_weights(raw, n_batch, wv):
    joints, verts = raw.shape
    jl = joints // n_batch
    w = raw[...].astype(F32)
    w = (w / jnp.sum(w, axis=0, keepdims=True)).astype(BF16).astype(F32)
    for q in range(4):
        parts = []
        for i in range(n_batch):
            if q > 0:
                parts.append(jnp.zeros((q * jl, verts), F32))
            parts.append(w[i * jl:(i + 1) * jl])
            if q < 3:
                parts.append(jnp.zeros(((3 - q) * jl, verts), F32))
        if 4 * joints < LANES:
            parts.append(jnp.zeros((LANES - 4 * joints, verts), F32))
        wv[q] = jnp.concatenate(parts, axis=0).astype(BF16)


def shape_rows(coefs, basis, te, n):
    k = basis.shape[1]
    cols = slice(n * WIDE, (n + 1) * WIDE)
    return [
        jnp.dot(coefs[:, :k], basis[e, :, cols], preferred_element_type=F32) + te[e:e + 1, cols].astype(F32)
        for e in range(3)
    ]


def skin_rows(step, shaped_of, poses, wv, put):
    verts = wv.shape[2]
    for n in range(verts // WIDE):
        cols = slice(n * WIDE, (n + 1) * WIDE)
        shaped = shaped_of(n)
        for d in range(3):
            total = jnp.dot(poses[d], wv[3, :, cols], preferred_element_type=F32)
            for e in range(3):
                total = total + shaped[e] * jnp.dot(poses[d], wv[e, :, cols], preferred_element_type=F32)
            for h in range(WIDE // LANES):
                t = n * (WIDE // LANES) + h
                put(d, 8 * (t % 2) + t // 2 + 2 * step, total[:, h * LANES:(h + 1) * LANES])


WHEN = {
    "even": {2: (0, 1, 2, 3, 4, 5), 1: (4, 5, 6, 8, 8, 10), 3: (16, 16, 16, 18, 18, 18)},
    "odd": {2: (0, 1, 2, 3, 4, 5), 1: (1, 2, 3, 4, 5, 5), 3: (8, 8, 10, 10, 12, 12)},
    "even wrap": {2: (4, 5, 5, 6, 6, 6), 1: (8, 8, 8, 10, 11, 11), 3: (14, 14, 16, 16, 18, 18)},
    "odd wrap": {2: (3, 4, 5, 6, 6, 6), 1: (1, 2, 3, 4, 5, 5), 3: (14, 14, 16, 16, 18, 18)},
}


def takes_before(at, chunks, count):
    found = {}
    for kind, slots in WHEN.items():
        for slot, times in slots.items():
            for p in range(count):
                if times[p * 6 // count] * chunks // 6 == at:
                    found.setdefault((slot, p), []).append(kind)
    return sorted(found.items(), key=lambda item: ((2, 1, 3).index(item[0][0]), item[0][1]))


def front_kernel(
    n_blk, n_batch, co_ref, tr_ref, ba_ref, te_ref, we_ref,
    mix, co_t, po_t, bas, tes, wv_last,
    cov, stage, packed, trv, wes, wv, early_shape,
    tr_send, tr_recv, bl_send, bl_recv, fw_send, fw_recv, own_sem,
):
    blk, bat = lax.axis_index("blk"), lax.axis_index("batch")
    sibling = bat + 1 - 2 * lax.rem(bat, 2)
    odd = lax.rem(blk, 2)
    pair = blk + 1 - 2 * odd
    after = lax.rem(blk + 2, n_blk)
    before = lax.rem(blk + n_blk - 2, n_blk)
    chars = trv.shape[3]
    chunks = chars // ROWS
    jl = stage.shape[1]
    k = cov.shape[0]
    verts = bas.shape[3]
    half = verts // 2

    own = [
        pltpu.make_async_copy(we_ref, wes.at[0], own_sem.at[0]),
        pltpu.make_async_copy(te_ref, tes.at[0], own_sem.at[1]),
        pltpu.make_async_copy(ba_ref, bas.at[0], own_sem.at[2]),
        pltpu.make_async_copy(tr_ref, stage, own_sem.at[3]),
        pltpu.make_async_copy(co_ref, cov, own_sem.at[4]),
    ]

    partners = [lax.rem(bat + i, n_batch) for i in range(1, n_batch)]
    barrier = pltpu.get_barrier_semaphore()
    for q in partners:
        pl.semaphore_signal(barrier, inc=1, device_id={"blk": blk, "batch": q})
    for b in (pair, before):
        pl.semaphore_signal(barrier, inc=1, device_id={"blk": b, "batch": bat})
    for c in own:
        c.start()

    mine = pl.ds(pl.multiple_of(lax.rem(bat, 2) * half, LANES), half)
    pieces = []
    for e in range(3):
        for low in range(0, k, CUT):
            pieces.append([(bas, e, pl.ds(low, min(CUT, k - low)))])
    pieces[0] = [tes, wes] + pieces[0]
    count = len(pieces)

    def part(entry, slot):
        if isinstance(entry, tuple):
            return entry[0].at[slot, entry[1], entry[2], mine]
        return entry.at[slot, :, mine]

    def kind_of(piece, i):
        return i if piece == 0 else 2

    def hop(slot_from, slot_to, piece, where, send, recv, target, shared=False):
        made = []
        for i, entry in enumerate(pieces[piece]):
            kind = kind_of(piece, i)
            at = kind if shared or kind < 2 else piece + 2
            made.append(pltpu.make_async_remote_copy(
                src_ref=part(entry, slot_from), dst_ref=part(entry, slot_to),
                send_sem=send.at[where, kind], recv_sem=recv.at[slot_to - 1, at],
                device_id={"blk": target[0], "batch": target[1]},
            ))
        return made

    def all_pieces(where, send, recv, slot):
        return [
            pltpu.make_async_remote_copy(
                src_ref=ref, dst_ref=ref, send_sem=send.at[where, kind], recv_sem=recv.at[slot - 1, kind],
                device_id={"blk": blk, "batch": sibling},
            )
            for kind, ref in enumerate(
                (tes.at[slot, :, mine], wes.at[slot, :, mine], bas.at[slot, :, :, mine])
            )
        ]

    def start(copies):
        for c in copies:
            c.start()

    def first_hop(piece):
        return hop(0, 2, piece, 1, bl_send, bl_recv, (after, bat))

    def to_odd(piece):
        return hop(0, 1, piece, 0, bl_send, bl_recv, (pair, bat))

    def across(piece):
        return hop(2, 3 - 2 * odd, piece, 2, bl_send, bl_recv, (pair, bat))

    def onward(piece):
        return hop(1, 3, piece, 3, bl_send, bl_recv, (after, bat))

    def share(slot, piece):
        return hop(slot, slot, piece, slot - 1, fw_send, fw_recv, (blk, sibling), shared=True)

    wrap = blk < 2
    is_kind = {
        "even": jnp.logical_and(odd == 0, jnp.logical_not(wrap)),
        "odd": jnp.logical_and(odd == 1, jnp.logical_not(wrap)),
        "even wrap": jnp.logical_and(odd == 0, wrap),
        "odd wrap": jnp.logical_and(odd == 1, wrap),
    }

    def take(slot, piece, kinds):
        def body():
            for c in hop(slot, slot, piece, slot - 1, bl_send, bl_recv, (pair, bat)):
                c.wait_recv()
            if slot == 2:
                start(across(piece))
            if slot == 1:
                @pl.when(odd == 0)
                def _():
                    start(onward(piece))
            start(share(slot, piece))

        if len(kinds) == len(is_kind):
            body()
        else:
            pl.when(functools.reduce(jnp.logical_or, [is_kind[x] for x in kinds]))(body)

    def got(slot, kinds):
        copies = all_pieces(slot - 1, fw_send, fw_recv, slot)
        for kind in kinds:
            copies[kind].wait_recv()

    moves = [[] for _ in range(chunks)]
    for c in range(chunks):
        for i, q in enumerate(partners):
            moves[c].append(pltpu.make_async_remote_copy(
                src_ref=packed.at[i, :, :, pl.ds(c * ROWS, ROWS)],
                dst_ref=trv.at[bat, :, :, pl.ds(c * ROWS, ROWS)],
                send_sem=tr_send.at[i], recv_sem=tr_recv.at[c],
                device_id={"blk": blk, "batch": q},
            ))

    def wide_move(i, count, cols):
        ref = trv.at[pl.ds(0, count), :, :, cols]
        return pltpu.make_async_remote_copy(
            src_ref=ref, dst_ref=ref, send_sem=tr_send.at[i], recv_sem=tr_recv.at[cols.start // ROWS],
            device_id={"blk": blk, "batch": partners[i]},
        )


    for c in own[:3]:
        c.wait()
    pl.semaphore_wait(barrier, len(partners) + 2)
    for p in range(count):
        start(first_hop(p))

    @pl.when(odd == 0)
    def _():
        for p in range(count):
            start(to_odd(p))

    own[3].wait()
    for i, q in enumerate(partners + [bat]):
        for c in range(chunks):
            cols = pl.ds(pl.multiple_of(q * chars + c * ROWS, LANES), ROWS)
            for d in range(3):
                rows = jnp.concatenate(
                    [stage[4 * d + e, :, cols].astype(F32) for e in range(4)], axis=0
                ).astype(BF16)
                if i < n_batch - 1:
                    packed[i, d, :, c * ROWS:(c + 1) * ROWS] = rows
                else:
                    trv[bat, d, :, c * ROWS:(c + 1) * ROWS] = rows

    for c in range(chunks):
        start(moves[c])

    place_weights(wes.at[0], n_batch, wv.at[0])
    own[4].wait()
    rest = jnp.zeros((LANES - k, ROWS), F32)
    for c in range(chunks):
        block = jnp.concatenate([cov[:, c * ROWS:(c + 1) * ROWS].astype(F32), rest], axis=0)
        co_t[c] = block.T.astype(BF16)
    for c in range(chunks):
        for n in range(verts // WIDE):
            for e, value in enumerate(shape_rows(co_t[c], bas.at[0], tes.at[0], n)):
                early_shape[c, n, e] = value

    def turn(c):
        for d in range(3):
            parts = [trv[i, d, :, c * ROWS:(c + 1) * ROWS].astype(F32) for i in range(n_batch)]
            if 4 * n_batch * jl < LANES:
                parts.append(jnp.zeros((LANES - 4 * n_batch * jl, ROWS), F32))
            po_t[d, c] = jnp.concatenate(parts, axis=0).T.astype(BF16)

    def unit(step, c, shaped_of=None):
        def put(d, at, value):
            mix[d, c, pl.ds(at, ROWS, stride=PITCH), :] = value

        def fresh(n):
            return shape_rows(co_t[c], bas.at[step], tes.at[step], n)

        skin_rows(step, shaped_of or fresh, [po_t[d, c] for d in range(3)], wv.at[step], put)

    def early(c):
        wide_move(0, n_batch - 1, slice(c * ROWS, (c + 1) * ROWS)).wait_recv()
        turn(c)
        unit(0, c, lambda n: [early_shape[c, n, e] for e in range(3)])

    order = (2 - odd, 1 + odd)
    for at in range(3 * chunks + 1):
        for (slot, piece), kinds in takes_before(at, chunks, count):
            take(slot, piece, kinds)
        turn_of, c = at // chunks, at % chunks
        if turn_of < 2 and c == chunks - 1:
            got(order[turn_of], (0, 1))
            place_weights(wes.at[order[turn_of]], n_batch, wv.at[order[turn_of]])
        if turn_of == 2 and c == chunks - 1:
            got(LAST, (0, 1))
            place_weights(wes.at[LAST], n_batch, wv_last)
        if turn_of == 0:
            early(c)
        if turn_of > 0 and c == 0:
            got(order[turn_of - 1] if turn_of < 3 else LAST, (2,))
        if 0 < turn_of < 3:
            unit(order[turn_of - 1], c)

    for i in range(n_batch - 1):
        wide_move(i, 1, slice(0, chars)).wait_send()
    for slot in (2, 1, 3):
        for c in all_pieces(slot - 1, fw_send, fw_recv, slot):
            c.wait_send()
    for where in (1, 2):
        for c in all_pieces(where, bl_send, bl_recv, 1):
            c.wait_send()

    @pl.when(odd == 0)
    def _():
        for where in (0, 3):
            for c in all_pieces(where, bl_send, bl_recv, 1):
                c.wait_send()


def front(n_blk, n_batch, coefficients, transforms, basis, template, weights):
    comps, jl, total = transforms.shape
    chars = total // n_batch
    chunks = chars // ROWS
    k = coefficients.shape[0]
    verts = weights.shape[1]
    joints = weights.shape[0]
    hop = STEPS - 1
    assert n_blk % 2 == 0 and n_blk > STEPS and n_batch % 2 == 0 and STEPS == 4
    assert chars % ROWS == 0 and k <= LANES and comps == 12
    assert joints == n_batch * jl and 4 * joints <= LANES
    sems = 3 * -(-k // CUT) + 2
    dma = pltpu.SemaphoreType.DMA
    any_spec = pl.BlockSpec(memory_space=pl.ANY)
    vmem_spec = pl.BlockSpec(memory_space=pltpu.VMEM)
    inputs = [
        pltpu.with_memory_space_constraint(a, pltpu.HBM)
        for a in (coefficients, transforms, basis, template, weights)
    ]
    return pl.pallas_call(
        functools.partial(front_kernel, n_blk, n_batch),
        out_shape=(
            pltpu.VMEM((3, chunks, ROWS * PITCH, LANES), F32),
            pltpu.VMEM((chunks, ROWS, LANES), BF16),
            pltpu.VMEM((3, chunks, ROWS, LANES), BF16),
            pltpu.VMEM((STEPS,) + basis.shape, BF16),
            pltpu.VMEM((STEPS,) + template.shape, BF16),
            pltpu.VMEM((4, LANES, verts), BF16),
        ),
        in_specs=[any_spec] * 5,
        out_specs=(vmem_spec,) * 6,
        scratch_shapes=[
            pltpu.VMEM((k, chars), BF16),
            pltpu.VMEM(transforms.shape, BF16),
            pltpu.VMEM((n_batch - 1, 3, 4 * jl, chars), BF16),
            pltpu.VMEM((n_batch, 3, 4 * jl, chars), BF16),
            pltpu.VMEM((STEPS,) + weights.shape, BF16),
            pltpu.VMEM((hop, 4, LANES, verts), BF16),
            pltpu.VMEM((chunks, verts // WIDE, 3, ROWS, WIDE), F32),
            dma((n_batch - 1,)), dma((chunks,)),
            dma((hop + 1, 3)), dma((hop, sems)), dma((hop, 3)), dma((hop, 3)), dma((5,)),
        ],
        compiler_params=pltpu.CompilerParams(
            collective_id=0, has_side_effects=True, vmem_limit_bytes=20 << 20
        ),
        cost_estimate=pl.CostEstimate(flops=0, bytes_accessed=20 << 20, transcendentals=0),
        name="front",
    )(*inputs)


def back_kernel(mix_in, co_t, po_t, bas, tes, wv, out_ref, mix, staged, sem):
    chunks = co_t.shape[0]
    part = ROWS // PARTS

    def send(c, p):
        return pltpu.make_async_copy(
            staged.at[c, pl.ds(p * part, part)], out_ref.at[pl.ds(c * ROWS + p * part, part)], sem.at[c, p]
        )

    def pack(c, p):
        for r in range(p * part, (p + 1) * part):
            for d in range(3):
                low = mix[d, c, pl.ds(r * PITCH, 8, stride=2), :]
                high = mix[d, c, pl.ds(r * PITCH + 1, 8, stride=2), :]
                staged[c, r, d] = jnp.concatenate([low, high], axis=0).astype(BF16)

    for c in range(chunks):
        def put(d, at, value):
            mix[d, c, pl.ds(at, ROWS, stride=PITCH), :] = value

        skin_rows(
            LAST, lambda n: shape_rows(co_t[c], bas.at[LAST], tes.at[LAST], n),
            [po_t[d, c] for d in range(3)], wv, put,
        )
        if c > 0:
            for p in range(PARTS):
                pack(c - 1, p)
            for p in range(PARTS):
                send(c - 1, p).start()
    for p in range(PARTS):
        pack(chunks - 1, p)
        send(chunks - 1, p).start()
    for c in range(chunks):
        for p in range(PARTS):
            send(c, p).wait()


def back(mix, co_t, po_t, bas, tes, wv):
    chunks = co_t.shape[0]
    chars = chunks * ROWS
    verts = wv.shape[2]
    group = (verts // LANES) * STEPS
    any_spec = pl.BlockSpec(memory_space=pl.ANY)
    vmem_spec = pl.BlockSpec(memory_space=pltpu.VMEM)
    out, _ = pl.pallas_call(
        back_kernel,
        out_shape=(
            jax.ShapeDtypeStruct((chars, 3, group, LANES), BF16),
            pltpu.VMEM(mix.shape, F32),
        ),
        in_specs=[vmem_spec] * 6,
        out_specs=(any_spec, vmem_spec),
        input_output_aliases={0: 1},
        scratch_shapes=[
            pltpu.VMEM((chunks, ROWS, 3, group, LANES), BF16),
            pltpu.SemaphoreType.DMA((chunks, PARTS)),
        ],
        compiler_params=pltpu.CompilerParams(vmem_limit_bytes=20 << 20),
        name="back",
    )(mix, co_t, po_t, bas, tes, wv)
    out = out.reshape(chars, 3, verts // LANES, STEPS, LANES)
    return out.transpose(0, 3, 1, 2, 4).reshape(chars, STEPS, 3, verts)


def solution(mesh):
    n_blk, n_batch = mesh.shape["blk"], mesh.shape["batch"]

    def per_device(coefficients, transforms, basis, template, skin_weights):
        basis = jnp.transpose(basis, (1, 0, 2))
        return back(*front(
            n_blk, n_batch, coefficients, transforms, basis, template, skin_weights
        ))

    in_specs = (
        P(None, ("blk", "batch")),
        P(None, "batch", "blk"),
        P(None, None, "blk"),
        P(None, "blk"),
        P(None, "blk"),
    )
    out_specs = P(("blk", "batch"), None, None, None)
    return jax.shard_map(
        per_device, mesh=mesh, in_specs=in_specs, out_specs=out_specs, check_vma=False
    )
```

time: 31.8 us -> 28.3 us (0.89)
  Pallas kernels: 31.5 us -> 28 us
    pallas_call x1, Pallas kernels: 24.8 us -> 22.6 us  [front(): pl.pallas_call(functools.partial(front_kernel, n_blk, n_batch), out_shape...]
    pallas_call x1, Pallas kernels: 6.66 us -> 5.35 us  [back(): pl.pallas_call(back_kernel, out_shape=(jax.ShapeDtypeStruct((chars, 3, gr...]
where the time goes in v2:
time: 28.3 us; the launch traced here: 28.2 us
  Pallas kernels  28 us (99%)
    pallas_call x1, Pallas kernels, front(): pl.pallas_call(functools.partial(front_kernel, n_blk, n_batch), out_shape...  22.6 us
    pallas_call x1, Pallas kernels, back(): pl.pallas_call(back_kernel, out_shape=(jax.ShapeDtypeStruct((chars, 3, gr...  5.35 us

profile of v2, /device:TPU:0, one launch (start us, length us, event | category | flops | bytes accessed | tf_op | source)
XLA Modules:
  0.0 28.2 jit_solution(17245902601545116728)
XLA Ops:
  0.0 22.6 %front.1 = (f32[3,6,2560,128]{3,2,1,0:T(8,128)S(1)}, bf16[6,128,128]{2,1,0:T(8,128)(2,1)S(1)}, bf16[3,6,128,128]{3,2,1,0:T(8,128)(2,1)S(1)}, bf16[4,3,120,512]{3...) custom-call(bf16[120,768]{1,0:T(8,128)(2,1)} %co_ref.1, ...), custom_call_target="tpu_custom_call" | custom-call | bytes 20971520 | tf_op jit(solution)/shard_map/front/pallas_call | solution.py:334
  22.6 5.4 %back.1 = (bf16[768,3,16,128]{3,2,1,0:T(8,128)(2,1)}, f32[3,6,2560,128]{3,2,1,0:T(8,128)S(1)}) custom-call(f32[3,6,2560,128]{3,2,1,0:T(8,128)S(1)} %get-tuple-element.12.mix_in, bf16[6,128,128]{2,1,0:T(8,128)(2,1)S(1)} %get-tuple-element.13.co_t, bf16[3,6,128,128]{3,2,1,0:T(8,128)(2,1)S(1)} %get-tuple-element.14.po_t, ...), custom_call_target="tpu_custom_call", output_to_operand_aliasing={{1}: (0, {})} | custom-call | tf_op jit(solution)/shard_map/back/pallas_call | solution.py:409

commit v3 on v2

--- a/solution.py
+++ b/solution.py
@@ -11,7 +11,7 @@
 WIDE = 256
 ROWS = 128
 PITCH = 20
-PARTS = 2
+PARTS = 4
 CUT = 64
 BF16 = jnp.bfloat16
 F32 = jnp.float32
@@ -60,10 +60,10 @@
 
 
 WHEN = {
-    "even": {2: (0, 1, 2, 3, 4, 5), 1: (4, 5, 6, 8, 8, 10), 3: (16, 16, 16, 18, 18, 18)},
-    "odd": {2: (0, 1, 2, 3, 4, 5), 1: (1, 2, 3, 4, 5, 5), 3: (8, 8, 10, 10, 12, 12)},
-    "even wrap": {2: (4, 5, 5, 6, 6, 6), 1: (8, 8, 8, 10, 11, 11), 3: (14, 14, 16, 16, 18, 18)},
-    "odd wrap": {2: (3, 4, 5, 6, 6, 6), 1: (1, 2, 3, 4, 5, 5), 3: (14, 14, 16, 16, 18, 18)},
+    "even": {2: (0, 1, 2, 3, 4, 5), 1: (3, 4, 5, 6, 8, 8), 3: (12, 16, 16, 16, 16, 16)},
+    "odd": {2: (0, 1, 1, 2, 3, 4), 1: (1, 2, 3, 4, 5, 5), 3: (8, 8, 10, 10, 12, 12)},
+    "even wrap": {2: (4, 5, 5, 6, 6, 6), 1: (8, 8, 10, 10, 11, 11), 3: (12, 16, 16, 16, 16, 16)},
+    "odd wrap": {2: (3, 4, 5, 6, 6, 6), 1: (1, 2, 3, 4, 5, 5), 3: (12, 16, 16, 16, 16, 16)},
 }
 
 
@@ -283,12 +283,17 @@
         for (slot, piece), kinds in takes_before(at, chunks, count):
             take(slot, piece, kinds)
         turn_of, c = at // chunks, at % chunks
-        if turn_of < 2 and c == chunks - 1:
+        if (turn_of, c) in ((0, chunks - 1), (1, chunks - 2)):
             got(order[turn_of], (0, 1))
             place_weights(wes.at[order[turn_of]], n_batch, wv.at[order[turn_of]])
-        if turn_of == 2 and c == chunks - 1:
+        if (turn_of, c) == (2, chunks - 2):
             got(LAST, (0, 1))
             place_weights(wes.at[LAST], n_batch, wv_last)
+            for i in range(n_batch - 1):
+                wide_move(i, 1, slice(0, chars)).wait_send()
+            for where in (1, 2):
+                for copy in all_pieces(where, bl_send, bl_recv, 1):
+                    copy.wait_send()
         if turn_of == 0:
             early(c)
         if turn_of > 0 and c == 0:
@@ -296,14 +301,9 @@
         if 0 < turn_of < 3:
             unit(order[turn_of - 1], c)
 
-    for i in range(n_batch - 1):
-        wide_move(i, 1, slice(0, chars)).wait_send()
     for slot in (2, 1, 3):
-        for c in all_pieces(slot - 1, fw_send, fw_recv, slot):
-            c.wait_send()
-    for where in (1, 2):
-        for c in all_pieces(where, bl_send, bl_recv, 1):
-            c.wait_send()
+        for copy in all_pieces(slot - 1, fw_send, fw_recv, slot):
+            copy.wait_send()
 
     @pl.when(odd == 0)
     def _():
@@ -366,9 +366,10 @@
     chunks = co_t.shape[0]
     part = ROWS // PARTS
 
-    def send(c, p):
+    def send(c, p=None):
+        low, size = (0, ROWS) if p is None else (p * part, part)
         return pltpu.make_async_copy(
-            staged.at[c, pl.ds(p * part, part)], out_ref.at[pl.ds(c * ROWS + p * part, part)], sem.at[c, p]
+            staged.at[c, pl.ds(low, size)], out_ref.at[pl.ds(c * ROWS + low, size)], sem.at[c, p or 0]
         )
 
     def pack(c, p):
@@ -389,14 +390,14 @@
         if c > 0:
             for p in range(PARTS):
                 pack(c - 1, p)
-            for p in range(PARTS):
-                send(c - 1, p).start()
+            send(c - 1).start()
     for p in range(PARTS):
         pack(chunks - 1, p)
         send(chunks - 1, p).start()
-    for c in range(chunks):
-        for p in range(PARTS):
-            send(c, p).wait()
+    for c in range(chunks - 1):
+        send(c).wait()
+    for p in range(PARTS):
+        send(chunks - 1, p).wait()
 
 
 def back(mix, co_t, po_t, bas, tes, wv):

time: 28.3 us -> 26.9 us (0.951)
  Pallas kernels: 28 us -> 26.6 us
    pallas_call x1, Pallas kernels: 22.6 us -> 21.2 us  [front(): pl.pallas_call(functools.partial(front_kernel, n_blk, n_batch), out_shape...]
where the time goes in v3:
time: 26.9 us; the launch traced here: 26.8 us
  Pallas kernels  26.6 us (99%)
    pallas_call x1, Pallas kernels, front(): pl.pallas_call(functools.partial(front_kernel, n_blk, n_batch), out_shape...  21.2 us
    pallas_call x1, Pallas kernels, back(): pl.pallas_call(back_kernel, out_shape=(jax.ShapeDtypeStruct((chars, 3, gr...  5.38 us

profile of v3, /device:TPU:0, one launch (start us, length us, event | category | flops | bytes accessed | tf_op | source)
XLA Modules:
  0.0 26.8 jit_solution(8941833939819443335)
XLA Ops:
  0.0 21.2 %front.1 = (f32[3,6,2560,128]{3,2,1,0:T(8,128)S(1)}, bf16[6,128,128]{2,1,0:T(8,128)(2,1)S(1)}, bf16[3,6,128,128]{3,2,1,0:T(8,128)(2,1)S(1)}, bf16[4,3,120,512]{3...) custom-call(bf16[120,768]{1,0:T(8,128)(2,1)} %co_ref.1, ...), custom_call_target="tpu_custom_call" | custom-call | bytes 20971520 | tf_op jit(solution)/shard_map/front/pallas_call | solution.py:334
  21.3 5.4 %back.1 = (bf16[768,3,16,128]{3,2,1,0:T(8,128)(2,1)}, f32[3,6,2560,128]{3,2,1,0:T(8,128)S(1)}) custom-call(f32[3,6,2560,128]{3,2,1,0:T(8,128)S(1)} %get-tuple-element.12.mix_in, bf16[6,128,128]{2,1,0:T(8,128)(2,1)S(1)} %get-tuple-element.13.co_t, bf16[3,6,128,128]{3,2,1,0:T(8,128)(2,1)S(1)} %get-tuple-element.14.po_t, ...), custom_call_target="tpu_custom_call", output_to_operand_aliasing={{1}: (0, {})} | custom-call | tf_op jit(solution)/shard_map/back/pallas_call | solution.py:410

commit v4 on v3

--- a/solution.py
+++ b/solution.py
@@ -12,7 +12,7 @@
 ROWS = 128
 PITCH = 20
 PARTS = 4
-CUT = 64
+CUT = 40
 BF16 = jnp.bfloat16
 F32 = jnp.float32
 LAST = STEPS - 1

time: 26.9 us -> 26.8 us (level)
  no operation moved by 1% of the time
where the time goes in v4:
time: 26.8 us; the launch traced here: 26.7 us
  Pallas kernels  26.5 us (99%)
    pallas_call x1, Pallas kernels, front(): pl.pallas_call(functools.partial(front_kernel, n_blk, n_batch), out_shape...  21.1 us
    pallas_call x1, Pallas kernels, back(): pl.pallas_call(back_kernel, out_shape=(jax.ShapeDtypeStruct((chars, 3, gr...  5.39 us

profile of v4, /device:TPU:0, one launch (start us, length us, event | category | flops | bytes accessed | tf_op | source)
XLA Modules:
  0.0 26.7 jit_solution(15514960057883411370)
XLA Ops:
  0.0 21.1 %front.1 = (f32[3,6,2560,128]{3,2,1,0:T(8,128)S(1)}, bf16[6,128,128]{2,1,0:T(8,128)(2,1)S(1)}, bf16[3,6,128,128]{3,2,1,0:T(8,128)(2,1)S(1)}, bf16[4,3,120,512]{3...) custom-call(bf16[120,768]{1,0:T(8,128)(2,1)} %co_ref.1, ...), custom_call_target="tpu_custom_call" | custom-call | bytes 20971520 | tf_op jit(solution)/shard_map/front/pallas_call | solution.py:334
  21.1 5.4 %back.1 = (bf16[768,3,16,128]{3,2,1,0:T(8,128)(2,1)}, f32[3,6,2560,128]{3,2,1,0:T(8,128)S(1)}) custom-call(f32[3,6,2560,128]{3,2,1,0:T(8,128)S(1)} %get-tuple-element.12.mix_in, bf16[6,128,128]{2,1,0:T(8,128)(2,1)S(1)} %get-tuple-element.13.co_t, bf16[3,6,128,128]{3,2,1,0:T(8,128)(2,1)S(1)} %get-tuple-element.14.po_t, ...), custom_call_target="tpu_custom_call", output_to_operand_aliasing={{1}: (0, {})} | custom-call | tf_op jit(solution)/shard_map/back/pallas_call | solution.py:410
